TPU v7x, 256 devices: a whole 4x4x8 slice. The times are simulated.
256 devices in a mesh: seq: 16 (over z, x_lo), img: 8 (over y, x_hi), fsdp: 2 (over core).
Axes of the slice: x: 4 (x_hi: 2, x_lo: 2; x = x_hi * 2 + x_lo), y: 4, z: 8, core: 2. Of those that a mesh axis runs over, the one named last changes fastest.
Arguments:
- vision_feats: bfloat16 [8, 2304, 1024], P('img', ('seq', 'fsdp')), may hold values from -6 to 6
- ln_gain: float32 [1024], replicated, may hold values from 0.5 to 1.5
- ln_bias: float32 [1024], replicated, may hold values from -3 to 3
- w_in: bfloat16 [1024, 4096], P('fsdp', 'seq'), may hold values from -0.1875 to 0.1875
- b_in: float32 [4096], P('seq'), may hold values from -3 to 3
- w_out: bfloat16 [4096, 4096], P('seq', 'fsdp'), may hold values from -0.09375 to 0.09375
- lm_grad: bfloat16 [8, 4096, 4096], P('img', 'seq', 'fsdp'), may hold values from -0.079589844 to 0.079589844
- image_counts: int32 [8, 2], P('img'), may hold values from 1 to 3, as said below
- token_pos: int32 [8, 2304], P('img'), may hold values from 0 to 2047, as said below
Outputs:
- w_in_grad: float32 [1024, 4096], P(('img', 'fsdp'), 'seq')
- b_in_grad: float32 [4096], replicated
- w_out_grad: float32 [4096, 4096], P(('seq', 'img'), 'fsdp')
- b_out_grad: float32 [4096], replicated
- ln_gain_grad: float32 [1024], replicated
- ln_bias_grad: float32 [1024], replicated
Inputs may be any that keep to these rules, and one draw needn't show every extreme that they name: `image_counts`: in each group the 2 samples hold 4 images together, each sample one or more. `token_pos`: each image's 576 tokens take consecutive positions of its sample's sequence in order; a sample's images come in order without intersection, and images are numbered sample by sample as image_counts gives.
All inputs are finite; a program needn't handle non-finite values.
Results may differ from a plain program's by a relative error of at most 0.0047.
Values may be sent and summed in bfloat16 or wider, within the bound.
No kernel may reach another device: no remote copies, remote signals or barrier semaphores. Data moves between devices by JAX's collectives and lax.ppermute only.
A program may use at most 128 MiB of HBM per device.

v0:
```python
import jax
import jax.numpy as jnp
from jax import lax
from jax.sharding import Mesh
from jax.sharding import PartitionSpec as P

PATCH = 576
LEN = 2048
SEQ = ("seq_0", "seq_1")
IMG = ("img_0", "img_1")
SEQ_FSDP = ("seq_0", "seq_1", "fsdp")
SEQ_IMG_FSDP = ("seq_0", "seq_1", "img_0", "img_1", "fsdp")
IMG_FSDP = ("img_0", "img_1", "fsdp")
SEQ_IMG = ("seq_0", "seq_1", "img_0", "img_1")


def copy_for_each(array, axis):
    copies = jnp.broadcast_to(array, (lax.axis_size(axis), *array.shape))
    return lax.all_to_all(copies, axis, split_axis=0, concat_axis=0, tiled=True)


def in_order(pieces, dim):
    shape = list(pieces.shape[1:])
    shape[dim] *= pieces.shape[0]
    return jnp.moveaxis(pieces, 0, dim).reshape(shape)


def gather_directly(array, axis, dim):
    pieces = copy_for_each(array, axis)
    return in_order(pieces, dim)


def whole_of(array, axes, dim):
    if not axes:
        return array
    nearer = lax.all_gather(array, axes[-1], axis=dim, tiled=True)
    return whole_of(nearer, axes[:-1], dim)


def taken_together(array, axis):
    return copy_for_each(array, axis).sum(axis=0)


def in_blocks(array, dim, devices):
    shape = array.shape
    pieces = array.reshape(*shape[:dim], devices, shape[dim] // devices, *shape[dim + 1 :])
    return jnp.moveaxis(pieces, dim, 0)


def one_scatter(arrays, axis, dims):
    devices = lax.axis_size(axis)
    pieces = [in_blocks(a, dim, devices) for a, dim in zip(arrays, dims)]
    lines = jnp.concatenate([b.reshape(devices, -1) for b in pieces], axis=1)
    width = max(16, -(-lines.shape[1] // 1024) * 8)
    lines = jnp.pad(lines, ((0, 0), (0, width * 128 - lines.shape[1]))).reshape(-1, 128)
    vector, at, gathered = (lax.psum_scatter(lines, axis, tiled=True).reshape(-1), 0, [])
    for b in pieces:
        part = b[0]
        gathered.append(vector[at : at + part.size].reshape(part.shape))
        at += part.size
    return tuple(gathered)


def one_axis_at_a_time(array, axes):
    for axis in axes:
        array = lax.psum(array, axis)
    return array


def gelu_parts(preact):
    cumul = 0.5 * (1.0 + lax.erf(preact * 0.7071067811865476))
    density = jnp.exp(-0.5 * preact * preact) * 0.3989422804014327
    return (preact * cumul, cumul + preact * density)


def contract(left, right, left_dim, right_dim):
    return lax.dot_general(
        left, right, (((left_dim,), (right_dim,)), ((), ())), preferred_element_type=jnp.float32
    )


def own_columns(matrix, img_count, fsdp_count, fsdp_index):
    rows = matrix.shape[0]
    block = matrix.shape[1] // (img_count * fsdp_count)
    shaped = matrix.reshape(rows, img_count, fsdp_count, block)
    taken = lax.dynamic_index_in_dim(shaped, fsdp_index, axis=2, keepdims=False)
    return taken.reshape(rows, img_count * block)


def place_columns(vector, img_count, fsdp_count, fsdp_index):
    block = vector.shape[0] // img_count
    holder = jnp.zeros((img_count, fsdp_count, block), jnp.float32)
    holder = lax.dynamic_update_slice(
        holder, vector.reshape(img_count, 1, block), (0, fsdp_index, 0)
    )
    return holder.reshape(img_count * fsdp_count * block)


def per_device(vision_feats, ln_gain, ln_bias, w_in, b_in, w_out, lm_grad, image_counts, token_pos):
    seq_count = lax.axis_size(SEQ)
    seq_index = lax.axis_index(SEQ)
    img_count = lax.axis_size(IMG)
    fsdp_count = lax.axis_size("fsdp")
    fsdp_index = lax.axis_index("fsdp")
    lm_block = lm_grad[0]
    block_rows = lm_block.shape[0]
    half_width = lm_block.shape[1]
    position_count = block_rows * seq_count
    counts = image_counts[0]
    positions = token_pos[0]
    row_count = positions.shape[0]
    image_index = jnp.arange(row_count, dtype=jnp.int32) // PATCH
    bounds = jnp.cumsum(counts)
    sample = jnp.sum((image_index[:, None] >= bounds[None, :]).astype(jnp.int32), axis=1)
    abs_pos = sample * LEN + positions
    marker = jnp.zeros((position_count,), jnp.float32).at[abs_pos].set(1.0)
    own_mask = lax.dynamic_slice_in_dim(marker, seq_index * block_rows, block_rows).astype(
        jnp.bfloat16
    )
    out_bias_half = jnp.dot(own_mask[None, :], lm_block, preferred_element_type=jnp.float32)[0]
    out_bias_full = lax.dynamic_update_slice_in_dim(
        jnp.zeros((half_width * fsdp_count,), jnp.float32),
        out_bias_half,
        fsdp_index * half_width,
        0,
    )
    w_in_full = gather_directly(w_in, "fsdp", 0)
    gathered = lax.all_gather(vision_feats[0], SEQ_FSDP, axis=0, tiled=True)
    values = gathered.astype(jnp.float32)
    row_mean = jnp.mean(values, axis=1, keepdims=True)
    centred = values - row_mean
    row_var = jnp.mean(centred * centred, axis=1, keepdims=True)
    normed = centred * lax.rsqrt(row_var + 1e-05)
    normed_in = (normed * ln_gain + ln_bias).astype(jnp.bfloat16)
    preact = jnp.dot(normed_in, w_in_full, preferred_element_type=jnp.float32) + b_in
    activ, slope = gelu_parts(preact)
    hidden = activ.astype(jnp.bfloat16)
    hidden_width = hidden.shape[1]
    whole_grad = whole_of(lm_block, SEQ, 0)
    picked = whole_grad[abs_pos]
    hidden_part = contract(picked, w_out, 1, 1)
    w_out_part = contract(hidden, picked, 0, 0)
    hidden_grad = taken_together(hidden_part, "fsdp")
    preact_grad = (hidden_grad * slope).astype(jnp.bfloat16)
    own_normed_in = own_columns(normed_in, img_count, fsdp_count, fsdp_index)
    own_normed = own_columns(normed, img_count, fsdp_count, fsdp_index)
    own_w_in = own_columns(w_in_full.T, img_count, fsdp_count, fsdp_index)
    w_in_part = contract(own_normed_in, preact_grad, 0, 0)
    half_rows = row_count // fsdp_count
    own_rows = lax.dynamic_slice_in_dim(preact_grad, fsdp_index * half_rows, half_rows, 0)
    b_in_part = jnp.sum(own_rows, axis=0, dtype=jnp.float32)
    normed_grad = contract(preact_grad, own_w_in, 1, 0)
    gain_part = place_columns(
        jnp.sum(normed_grad * own_normed, axis=0), img_count, fsdp_count, fsdp_index
    )
    bias_part = place_columns(jnp.sum(normed_grad, axis=0), img_count, fsdp_count, fsdp_index)
    w_in_grad, w_out_grad = one_scatter((w_in_part, w_out_part), IMG, (0, 0))
    hidden_full = lax.dynamic_update_slice_in_dim(
        jnp.zeros((hidden_width * seq_count,), jnp.float32), b_in_part, seq_index * hidden_width, 0
    )
    gain_grad, bias_grad, b_in_grad, b_out_grad = (
        one_axis_at_a_time(gain_part, SEQ_IMG_FSDP),
        one_axis_at_a_time(bias_part, SEQ_IMG_FSDP),
        one_axis_at_a_time(hidden_full, SEQ_IMG_FSDP),
        one_axis_at_a_time(out_bias_full, SEQ_IMG_FSDP),
    )
    return (w_in_grad, b_in_grad, w_out_grad, b_out_grad, gain_grad, bias_grad)


def solution(mesh):
    finer = Mesh(
        mesh.devices.reshape(8, 2, 4, 2, mesh.shape["fsdp"]),
        ("seq_0", "seq_1", "img_0", "img_1", "fsdp"),
    )
    placed = (
        P(IMG, SEQ_FSDP, None),
        P(),
        P(),
        P("fsdp", SEQ),
        P(SEQ),
        P(SEQ, "fsdp"),
        P(IMG, SEQ, "fsdp"),
        P(IMG, None),
        P(IMG, None),
    )
    return jax.shard_map(
        per_device,
        mesh=finer,
        in_specs=placed,
        out_specs=(P(IMG_FSDP, SEQ), P(), P(SEQ_IMG, "fsdp"), P(), P(), P()),
        check_vma=False,
    )
```

profile of v0, /device:TPU:1, one launch (start us, length us, event | category | flops | bytes accessed | tf_op | source)
XLA Modules:
  0.0 471.8 jit_solution(9273449355537463096)
XLA Ops:
  7.2 0.0 copy-start
  7.2 0.0 copy-start.13
  7.2 0.0 copy-start.9
  7.2 0.0 all-gather.9.cloned.1.call-start
  7.3 0.7 all-gather.9.cloned.1.call-update
  7.9 0.0 all-gather.7.cloned.1.call-start
  8.0 0.7 all-gather.7.cloned.1.call-update
  8.7 0.0 all-gather.11.cloned.1.call-start
  8.7 42.9 %all-gather.9.cloned.1.call-done = bf16[1,512,2048]{2,1,0:T(8,128)(2,1)} async-done(((bf16[1,256,2048]{2,1,0:T(8,128)(2,1)}), bf16[1,512,2048]{2,1,0:T(8,128)(2,1)}) %all-gather.9.cloned.1.call-update) | async-done | bytes 2097168 | tf_op jit(solution)/shard_map/all_gather | solution.py:36
  51.6 0.0 all-gather.11.cloned.1.call-update
  51.7 0.2 reduce-window.8
  51.9 0.1 fusion.13
  52.0 70.0 %all-gather.7.cloned.1.call-done = bf16[1,2304,1024]{2,1,0:T(8,128)(2,1)} async-done(((bf16[1,72,1024]{2,1,0:T(8,128)(2,1)}), bf16[1,2304,1024]{2,1,0:T(8,128)(2,1)}) %all-gather.7.cloned.1.call-update) | async-done | bytes 4718608 | tf_op jit(solution)/shard_map/all_gather | solution.py:128
  122.1 6.8 %copy.20 = bf16[1,2304,1024]{1,2,0:T(8,128)(2,1)} copy(bf16[1,2304,1024]{2,1,0:T(8,128)(2,1)} %all-gather.7.cloned.1.call-done) | data formatting | bytes 9437184 | tf_op jit(solution)/shard_map/all_gather | solution.py:128
  128.9 3.2 convert_reduce_fusion
  132.1 0.6 copy-done.2
  132.6 1.3 fusion.3
  133.9 4.8 %fusion.1 = (f32[2304,1024]{0,1:T(8,128)}, bf16[2304,1024]{0,1:T(8,128)(2,1)S(1)}) fusion(bf16[1,2304,1024]{1,2,0:T(8,128)(2,1)S(1)} %copy-done.2, f32[2304]{0:T(1024)S(1)} %add_rsqrt_fusion, f32[2304]{0:T(1024)S(1)} %broadcast_multiply_fusion.1, f32[1024]{0:T(1024)S(1)} %copy-done.10, f32[1024]{0:T(1024)S(1)} %copy-done.11), kind=kLoop, calls=%fused_computation.5 | loop fusion | flops 14155776 | bytes 18900992 | tf_op jit(solution)/shard_map/mul | solution.py:133
  138.7 2.1 copy-done.3
  140.9 1.6 constant_dynamic-slice_fusion.2
  142.5 153.5 %all-gather.11.cloned.1.call-done = bf16[1,4096,2048]{2,1,0:T(8,128)(2,1)} async-done(((bf16[1,512,2048]{2,1,0:T(8,128)(2,1)}), bf16[1,4096,2048]{2,1,0:T(8,128)(2,1)}) %all-gather.11.cloned.1.call-update) | async-done | bytes 16777232 | tf_op jit(solution)/shard_map/all_gather | solution.py:36
  296.0 26.2 %gather_fusion = bf16[2304,2048]{1,0:T(8,128)(2,1)} fusion(bf16[4096,2048]{1,0:T(8,128)(2,1)} %bitcast.43, s32[3072]{0:T(1024)S(1)} %pad_clamp_fusion), kind=kCustom, calls=%fused_computation | custom fusion | bytes 18883584 | tf_op jit(solution)/shard_map/gather | solution.py:140
  322.2 5.2 %fusion.21 = f32[2304,256]{1,0:T(8,128)S(1)} fusion(bf16[2304,2048]{1,0:T(8,128)(2,1)} %gather_fusion, bf16[256,2048]{1,0:T(8,128)(2,1)S(1)} %copy-done), kind=kOutput, calls=%fused_computation.48 | convolution fusion | flops 2415919104 | bytes 12845056 | tf_op jit(solution)/shard_map/dot_general | solution.py:77
  327.5 0.3 broadcast_in_dim.6
  327.8 0.0 copy-start.8
  327.8 9.2 %all_to_all.10 = f32[2,2304,256]{2,1,0:T(8,128)} all-to-all(f32[2,2304,256]{2,1,0:T(8,128)S(1)} %broadcast_in_dim.6), channel_id=1, replica_groups=mesh['seq_0'=8,'seq_1'=2,'img_0'=4,'img_1'=2,'fsdp'=2] {'fsdp'}, dimensions={0} | all-to-all | bytes 9437184 | tf_op jit(solution)/shard_map/all_to_all | solution.py:19
  337.0 0.0 copy-done.8
  337.0 0.8 broadcast_in_dim.7
  337.9 3.8 all-to-all-start.1
  341.7 0.0 reduce-scatter.2.cloned.1.call-start
  341.7 4.5 reduce_sum.66
  346.2 0.0 all-to-all-done.1
  346.2 0.0 slice-start.2
  346.2 6.7 %fusion.9 = (bf16[2304,256]{1,0:T(8,128)(2,1)}, f32[2304,256]{1,0:T(8,128)S(1)}) fusion(f32[2304,256]{1,0:T(8,128)} %reduce_sum.66, f32[256]{0:T(256)S(1)} %copy-done.12, bf16[2304,1024]{0,1:T(8,128)(2,1)} %copy-done.3, bf16[1024,256]{1,0:T(8,128)(2,1)S(1)} %bitcast.50), kind=kOutput, calls=%fused_computation.18 | convolution fusion | flops 1214447616 | bytes 11142144 | tf_op jit(solution)/shard_map/dot_general | solution.py:135
  352.9 4.0 fusion.10
  356.9 2.0 reshape_reshape.7
  358.9 2.8 fusion.22
  361.7 0.1 reshape_reshape.6
  361.8 1.7 pad_maximum_fusion
  363.5 3.6 reshape.151
  367.1 0.0 reduce-scatter.2.cloned.1.call-update
  367.1 9.0 %scatter_custom_fusion = f32[4096]{0:T(1024)S(1)} fusion(s32[2304]{0:T(1024)S(1)} %fusion.17, f32[2304]{0:T(1024)S(1)} %broadcast.81, f32[]{:T(128)} %constant.22.clone.1), kind=kCustom, calls=%fused_computation.39 | custom fusion | bytes 16388 | tf_op jit(solution)/shard_map/scatter | solution.py:116
  376.1 0.1 dynamic_slice.28
  376.2 0.0 copy-done.4
  376.2 0.2 fusion.11
  376.5 0.2 dynamic_update_slice.13
  376.7 5.0 %constant_dynamic-slice_fusion = f32[2304,8,1,64]{0,3,2,1:T(8,128)} fusion(f32[2304,8,2,64]{0,3,2,1:T(8,128)} %bitcast.46, s32[]{:T(128)S(6)} %select_n.40), kind=kLoop, calls=%fused_computation.44 | loop fusion | bytes 9437188 | tf_op jit(solution)/shard_map/jit(dynamic_index_in_dim)/dynamic_slice | solution.py:86
  381.8 6.2 %copy.21 = f32[2304,512]{1,0:T(8,128)} copy(f32[2304,512]{0,1:T(8,128)} %bitcast.47) | data formatting | bytes 9437184 | tf_op jit(solution)/shard_map/reshape | solution.py:87
  388.0 3.3 fusion.20
  391.3 0.1 reshape.158
  391.5 0.1 reshape.159
  391.5 0.1 reshape.160
  391.7 0.1 reshape.161
  391.7 0.2 convert_reduce_fusion.1
  391.9 0.3 dynamic_update_slice.12
  392.2 23.3 %all-reduce = (f32[4096]{0:T(1024)S(1)}, f32[4096]{0:T(1024)S(1)}, f32[1024]{0:T(1024)S(1)}, f32[1024]{0:T(1024)S(1)}) all-reduce(f32[4096]{0:T(1024)S(1)} %dynamic_update_slice.12, f32[4096]{0:T(1024)S(1)} %dynamic_update_slice.13, ...), channel_id=1, replica_groups=mesh['seq_0'=8,'seq_1'=2,'img_0'=4,'img_1'=2,'fsdp'=2] {'seq_0'}, use_global_device_ids=true, to_apply=%region_7.8 | all-reduce | flops 10240 | bytes 81920 | tf_op jit(solution)/shard_map/psum | solution.py:66
  415.5 5.9 %all-reduce.4 = (f32[4096]{0:T(1024)S(1)}, f32[4096]{0:T(1024)S(1)}, f32[1024]{0:T(1024)S(1)}, f32[1024]{0:T(1024)S(1)}) all-reduce(f32[4096]{0:T(1024)S(1)} %get-tuple-element.8, f32[4096]{0:T(1024)S(1)} %get-tuple-element.9, ...), channel_id=1, replica_groups=mesh['seq_0'=8,'seq_1'=2,'img_0'=4,'img_1'=2,'fsdp'=2] {'seq_1'}, use_global_device_ids=true, to_apply=%region_8.9 | all-reduce | flops 10240 | bytes 81920 | tf_op jit(solution)/shard_map/psum | solution.py:66
  421.4 14.4 %all-reduce.1 = (f32[4096]{0:T(1024)S(1)}, f32[4096]{0:T(1024)S(1)}, f32[1024]{0:T(1024)S(1)}, f32[1024]{0:T(1024)S(1)}) all-reduce(f32[4096]{0:T(1024)S(1)} %get-tuple-element.24, f32[4096]{0:T(1024)S(1)} %get-tuple-element.25, ...), channel_id=1, replica_groups=mesh['seq_0'=8,'seq_1'=2,'img_0'=4,'img_1'=2,'fsdp'=2] {'img_0'}, use_global_device_ids=true, to_apply=%region_9.10 | all-reduce | flops 10240 | bytes 81920 | tf_op jit(solution)/shard_map/psum | solution.py:66
  435.7 10.3 %all-reduce.3 = (f32[4096]{0:T(1024)S(1)}, f32[4096]{0:T(1024)S(1)}, f32[1024]{0:T(1024)S(1)}, f32[1024]{0:T(1024)S(1)}) all-reduce(f32[4096]{0:T(1024)S(1)} %get-tuple-element.12, f32[4096]{0:T(1024)S(1)} %get-tuple-element.13, ...), channel_id=1, replica_groups=mesh['seq_0'=8,'seq_1'=2,'img_0'=4,'img_1'=2,'fsdp'=2] {'img_1'}, use_global_device_ids=true, to_apply=%region_10.11 | all-reduce | flops 10240 | bytes 81920 | tf_op jit(solution)/shard_map/psum | solution.py:66
  446.0 16.1 %all-reduce.2 = (f32[4096]{0:T(1024)}, f32[4096]{0:T(1024)}, f32[1024]{0:T(1024)}, f32[1024]{0:T(1024)}) all-reduce(f32[4096]{0:T(1024)S(1)} %get-tuple-element.20, f32[4096]{0:T(1024)S(1)} %get-tuple-element.21, f32[1024]{0:T(1024)S(1)} %get-tuple-element.22, ...), channel_id=1, replica_groups=mesh['seq_0'=8,'seq_1'=2,'img_0'=4,'img_1'=2,'fsdp'=2] {'fsdp'}, use_global_device_ids=true, to_apply=%region_11.12 | all-reduce | flops 10240 | bytes 81920 | tf_op jit(solution)/shard_map/psum | solution.py:66
  462.1 0.8 slice.12
  462.9 0.6 reshape.152
  463.6 1.0 slice.13
  464.6 0.7 reshape.153
  (42 shorter events, 0.2 us)
Async XLA Ops:
  7.2 315.1 %copy-start = (bf16[256,2048]{1,0:T(8,128)(2,1)S(1)}, bf16[256,2048]{1,0:T(8,128)(2,1)}, u32[]{:S(2)}) copy-start(bf16[256,2048]{1,0:T(8,128)(2,1)} %param.14) | copy-start | bytes 3145732
  7.2 44.5 %copy-start.13 = (s32[1,2]{1,0:T(1,128)S(1)}, s32[1,2]{1,0:T(1,128)}, u32[]{:S(2)}) copy-start(s32[1,2]{1,0:T(1,128)} %param.16) | copy-start | bytes 28
  7.2 44.8 %copy-start.9 = (s32[1,2304]{1,0:T(1,128)S(1)}, s32[1,2304]{1,0:T(1,128)}, u32[]{:S(2)}) copy-start(s32[1,2304]{1,0:T(1,128)} %param.17) | copy-start | bytes 27652
  7.2 44.4 %all-gather.9.cloned.1.call-start = ((), (), s32[]{:S(2)}) async-start(), calls=%async_computation.5 | async-start | bytes 3145728 | tf_op jit(solution)/shard_map/all_gather | solution.py:36
  7.9 114.2 %all-gather.7.cloned.1.call-start = ((), (), s32[]{:S(2)}) async-start(), calls=%async_computation.4 | async-start | bytes 4866048 | tf_op jit(solution)/shard_map/all_gather | solution.py:128
  8.7 287.3 %all-gather.11.cloned.1.call-start = ((), (), s32[]{:S(2)}) async-start(), calls=%async_computation.6 | async-start | bytes 18874368 | tf_op jit(solution)/shard_map/all_gather | solution.py:36
  128.9 3.8 copy-start.2
  132.6 1.3 copy-start.10
  132.6 1.3 copy-start.11
  138.7 2.1 copy-start.3
  327.8 9.2 %copy-start.8 = (bf16[512,256]{1,0:T(8,128)(2,1)S(1)}, bf16[512,256]{1,0:T(8,128)(2,1)}, u32[]{:S(2)}) copy-start(bf16[512,256]{1,0:T(8,128)(2,1)} %param.12) | copy-start | bytes 786436
  337.9 8.3 %all-to-all-start.1 = ((bf16[2,512,256]{2,1,0:T(8,128)(2,1)}), bf16[2,512,256]{2,1,0:T(8,128)(2,1)S(1)}, u32[]{:S(2)}, u32[]{:S(2)}) async-start(bf16[2,512,256]{2,1,0:T(8,128)(2,1)} %broadcast_in_dim.7), calls=%async_computation.1 | async-start | bytes 1048576 | tf_op jit(solution)/shard_map/all_to_all | solution.py:19
  341.7 4.5 copy-start.12
  341.7 120.4 %reduce-scatter.2.cloned.1.call-start = ((), (), s32[]{:S(2)}) async-start(), calls=%async_computation.3 | async-start | bytes 2949120 | tf_op jit(solution)/shard_map/reduce_scatter | solution.py:56
  341.7 11.2 %slice-start = ((s8[9437184]{0:T(1024)(128)(4,1)}), s8[1048576]{0:T(1024)(128)(4,1)S(1)}, s32[]{:S(2)}) async-start(s8[9437184]{0:T(1024)(128)(4,1)} %bitcast.44), calls=%async_computation.7 | async-start | bytes 2097152
  346.2 6.7 %copy-start.6 = (bf16[2,512,256]{2,1,0:T(8,128)(2,1)}, bf16[2,512,256]{2,1,0:T(8,128)(2,1)S(1)}, u32[]{:S(2)}) copy-start(bf16[2,512,256]{2,1,0:T(8,128)(2,1)S(1)} %all-to-all-done.1) | copy-start | bytes 1572868
  346.2 6.7 %slice-start.1 = ((s8[9437184]{0:T(1024)(128)(4,1)}), s8[4194304]{0:T(1024)(128)(4,1)S(1)}, s32[]{:S(2)}) async-start(s8[9437184]{0:T(1024)(128)(4,1)} %bitcast.44), calls=%async_computation.8 | async-start | bytes 8388608
  346.2 6.7 %slice-start.2 = ((s8[9437184]{0:T(1024)(128)(4,1)}), s8[4194304]{0:T(1024)(128)(4,1)S(1)}, s32[]{:S(2)}) async-start(s8[9437184]{0:T(1024)(128)(4,1)} %bitcast.44), calls=%async_computation.9 | async-start | bytes 8388608
  367.1 9.1 %copy-start.4 = (bf16[1,256,2048]{2,1,0:T(8,128)(2,1)S(1)}, bf16[1,256,2048]{2,1,0:T(8,128)(2,1)}, u32[]{:S(2)}) copy-start(bf16[1,256,2048]{2,1,0:T(8,128)(2,1)} %param.15) | copy-start | bytes 3145732
  367.1 9.6 %copy-start.7 = (bf16[2,512,256]{2,1,0:T(8,128)(2,1)S(1)}, bf16[2,512,256]{2,1,0:T(8,128)(2,1)}, u32[]{:S(2)}) copy-start(bf16[2,512,256]{2,1,0:T(8,128)(2,1)} %copy-done.6) | copy-start | bytes 1572868
  381.8 6.3 %copy-start.5 = (bf16[2304,256]{1,0:T(8,128)(2,1)S(1)}, bf16[2304,256]{1,0:T(8,128)(2,1)}, u32[]{:S(2)}) copy-start(bf16[2304,256]{1,0:T(8,128)(2,1)} %get-tuple-element.30) | copy-start | bytes 3538948
  388.0 77.3 %copy-start.1 = (bf16[256,2048]{1,0:T(8,128)(2,1)S(1)}, bf16[256,2048]{1,0:T(8,128)(2,1)}, u32[]{:S(2)}) copy-start(bf16[256,2048]{1,0:T(8,128)(2,1)} %param.14) | copy-start | bytes 3145732
Sparse Core Ops, SparseCore 0:
  9.8 41.7 all-gather.8
  53.5 68.5 all-gather.6
  123.9 172.0 all-gather.10
  367.2 79.7 reduce-scatter.1
where the time goes:
time: 473 us; the launch traced here: 472 us
  waiting for transfers between devices  268 us (57%)
  blocking collectives  79.1 us (17%)
  local copies, waits for them, and re-layouts  68.7 us (15%)
  matrix products  22.2 us (5%)
  other arithmetic  16 us (3%)
  between operations  14 us (3%)
    all_gather x2, waiting for transfers between devices, whole_of(): nearer = lax.all_gather(array, axes[-1], axis=dim, tiled=True)  196 us
    all_gather x1, waiting for transfers between devices, per_device(): gathered = lax.all_gather(vision_feats[0], SEQ_FSDP, axis=0, tiled=True)  70 us
    psum x5, blocking collectives, one_axis_at_a_time(): array = lax.psum(array, axis)  69.9 us
    gather x1, local copies, waits for them, and re-layouts, per_device(): picked = whole_grad[abs_pos]  26.2 us
    dot_general x4, matrix products, contract(): lax.dot_general(left, right, (((left_dim,), (right_dim,)), ((), ())), pre...  15.2 us
  transfers between devices with their start and end apart: 5, of which 3 were waited for; matrix products, arithmetic and copies ran while one was open for 10% of the time, Pallas kernels for 0%

commit v1 on v0

--- a/solution.py
+++ b/solution.py
@@ -125,7 +125,10 @@
         0,
     )
     w_in_full = gather_directly(w_in, "fsdp", 0)
-    gathered = lax.all_gather(vision_feats[0], SEQ_FSDP, axis=0, tiled=True)
+    gathered = jnp.concatenate(
+        lax.all_to_all(jnp.stack([vision_feats[0]] * lax.axis_size(SEQ_FSDP)), SEQ_FSDP, 0, 0),
+        axis=0,
+    )
     values = gathered.astype(jnp.float32)
     row_mean = jnp.mean(values, axis=1, keepdims=True)
     centred = values - row_mean

time: 473 us -> 502 us (1.061)
  local copies, waits for them, and re-layouts: 68.7 us -> 101 us
  waiting for transfers between devices: 268 us -> 239 us
  other arithmetic: 16 us -> 32.6 us
  starting transfers between devices: 3.97 us -> 12.1 us
    all_to_all x0 -> x1, waiting for transfers between devices: none -> 157 us  [per_device(): lax.all_to_all(jnp.stack([vision_feats[0]] * lax.axis_size(SEQ_FSDP)), SE...]
    all_gather x2, waiting for transfers between devices: 196 us -> 81.1 us  [whole_of(): nearer = lax.all_gather(array, axes[-1], axis=dim, tiled=True)]
    all_gather x1 -> x0, waiting for transfers between devices: 70 us -> none  [per_device(): gathered = lax.all_gather(vision_feats[0], SEQ_FSDP, axis=0, tiled=True)]
    convert_element_type x0 -> x2, local copies, waits for them, and re-layouts: none -> 42.9 us  [per_device(): values = gathered.astype(jnp.float32)]
    convert_element_type x0 -> x2, other arithmetic: none -> 13.1 us  [per_device(): normed_in = (normed * ln_gain + ln_bias).astype(jnp.bfloat16)]
    all_to_all x0 -> x1, starting transfers between devices: none -> 8.2 us  [per_device(): lax.all_to_all(jnp.stack([vision_feats[0]] * lax.axis_size(SEQ_FSDP)), SE...]
    all_gather x1 -> x0, local copies, waits for them, and re-layouts: 6.78 us -> none  [per_device(): gathered = lax.all_gather(vision_feats[0], SEQ_FSDP, axis=0, tiled=True)]
    dynamic_slice x3 -> x2, local copies, waits for them, and re-layouts: 6.68 us -> 0.03 us  [own_columns(): taken = lax.dynamic_index_in_dim(shaped, fsdp_index, axis=2, keepdims=False)]
  transfers between devices with their start and end apart: 5 -> 5, of which waited for: 3 -> 3; matrix products, arithmetic and copies ran while one was open for 10% -> 19% of each run, Pallas kernels for 0% -> 0%
where the time goes in v1:
time: 502 us; the launch traced here: 500 us
  waiting for transfers between devices  239 us (48%)
  local copies, waits for them, and re-layouts  101 us (20%)
  blocking collectives  78.8 us (16%)
  other arithmetic  32.6 us (6%)
  matrix products  23.2 us (5%)
  between operations  14 us (3%)
  starting transfers between devices  12.1 us (2%)
    all_to_all x1, waiting for transfers between devices, per_device(): lax.all_to_all(jnp.stack([vision_feats[0]] * lax.axis_size(SEQ_FSDP)), SE...  157 us
    all_gather x2, waiting for transfers between devices, whole_of(): nearer = lax.all_gather(array, axes[-1], axis=dim, tiled=True)  81.1 us
    psum x5, blocking collectives, one_axis_at_a_time(): array = lax.psum(array, axis)  69.9 us
    convert_element_type x2, local copies, waits for them, and re-layouts, per_device(): values = gathered.astype(jnp.float32)  42.9 us
    gather x1, local copies, waits for them, and re-layouts, per_device(): picked = whole_grad[abs_pos]  26.3 us
    dot_general x4, matrix products, contract(): lax.dot_general(left, right, (((left_dim,), (right_dim,)), ((), ())), pre...  16.2 us
    convert_element_type x2, other arithmetic, per_device(): normed_in = (normed * ln_gain + ln_bias).astype(jnp.bfloat16)  13.1 us
  transfers between devices with their start and end apart: 5, of which 3 were waited for; matrix products, arithmetic and copies ran while one was open for 19% of the time, Pallas kernels for 0%

profile of v1, /device:TPU:1, one launch (start us, length us, event | category | flops | bytes accessed | tf_op | source)
XLA Modules:
  0.0 500.0 jit_solution(17388294014397632567)
XLA Ops:
  7.2 0.0 copy-start
  7.2 0.0 all-gather.5.cloned.1.call-start
  7.2 0.7 all-gather.5.cloned.1.call-update
  7.9 0.0 all-gather.7.cloned.1.call-start
  8.0 43.6 %all-gather.5.cloned.1.call-done = bf16[1,512,2048]{2,1,0:T(8,128)(2,1)} async-done(((bf16[1,256,2048]{2,1,0:T(8,128)(2,1)}), bf16[1,512,2048]{2,1,0:T(8,128)(2,1)}) %all-gather.5.cloned.1.call-update) | async-done | bytes 2097168 | tf_op jit(solution)/shard_map/all_gather | solution.py:36
  51.6 0.0 all-gather.7.cloned.1.call-update
  51.7 2.7 stack.3
  54.4 8.2 %all-to-all-start = ((bf16[32,72,1024]{2,1,0:T(8,128)(2,1)}), bf16[32,72,1024]{2,1,0:T(8,128)(2,1)}, u32[]{:S(2)}, u32[]{:S(2)}) async-start(bf16[32,72,1024]{2,1,0:T(8,128)(2,1)} %stack.3), calls=%async_computation | async-start | bytes 9437184 | tf_op jit(solution)/shard_map/all_to_all | solution.py:129
  62.6 0.2 reduce-window.8
  62.8 0.1 mul.106
  62.9 0.0 copy-done.8
  62.9 0.1 add.139
  63.0 0.1 fusion.9
  63.1 0.0 copy-done.10
  63.2 156.9 %all-to-all-done = bf16[32,72,1024]{2,1,0:T(8,128)(2,1)} async-done(((bf16[32,72,1024]{2,1,0:T(8,128)(2,1)}), bf16[32,72,1024]{2,1,0:T(8,128)(2,1)}, u32[]{:S(2)}, u32[]{:S(2)}) %all-to-all-start) | async-done | bytes 4718624 | tf_op jit(solution)/shard_map/all_to_all | solution.py:129
  220.0 3.1 convert_reduce_fusion
  223.2 0.1 div.19
  223.3 3.8 multiply_reduce_fusion
  227.1 0.1 rsqrt.13
  227.2 18.0 %reshape.252 = f32[2304,8,2,64]{3,2,1,0:T(2,128)} reshape(bf16[32,72,1024]{2,1,0:T(8,128)(2,1)} %all-to-all-done) | data formatting | bytes 14155776 | tf_op jit(solution)/shard_map/convert_element_type | solution.py:132
  245.2 24.9 %copy.21 = f32[2304,8,2,64]{0,3,2,1:T(8,128)} copy(f32[2304,8,2,64]{3,2,1,0:T(2,128)} %reshape.252) | data formatting | bytes 18874368 | tf_op jit(solution)/shard_map/convert_element_type | solution.py:132
  270.1 6.9 %add_convert_fusion = bf16[32,72,1024]{2,1,0:T(8,128)(2,1)} fusion(bf16[32,72,1024]{2,1,0:T(8,128)(2,1)} %all-to-all-done, f32[1024]{0:T(1024)S(1)} %copy-done.8, f32[1024]{0:T(1024)S(1)} %copy-done.9, f32[32,72]{1,0:T(8,128)S(1)} %add_rsqrt_fusion, f32[32,72]{1,0:T(8,128)S(1)} %broadcast_multiply_fusion), kind=kLoop, calls=%fused_computation.2 | loop fusion | flops 14155776 | bytes 9463808 | tf_op jit(solution)/shard_map/convert_element_type | solution.py:137
  277.0 4.8 subtract_multiply_fusion
  281.8 6.2 %add_convert_fusion.1 = (bf16[2304,8,1,64]{0,3,2,1:T(8,128)(2,1)}, f32[2304,8,1,64]{0,3,2,1:T(8,128)}) fusion(f32[8,1,64]{2,1,0:T(1,128)S(1)} %get-tuple-element.33, f32[8,1,64]{2,1,0:T(1,128)S(1)} %get-tuple-element.32, f32[2304,8,2,64]{0,3,2,1:T(8,128)} %subtract_multiply_fusion, s32[]{:T(128)S(6)} %select_n.40), kind=kLoop, calls=%fused_computation.7 | loop fusion | flops 3538944 | bytes 11800580 | tf_op jit(solution)/shard_map/convert_element_type | solution.py:137
  287.9 37.5 %all-gather.7.cloned.1.call-done = bf16[1,4096,2048]{2,1,0:T(8,128)(2,1)} async-done(((bf16[1,512,2048]{2,1,0:T(8,128)(2,1)}), bf16[1,4096,2048]{2,1,0:T(8,128)(2,1)}) %all-gather.7.cloned.1.call-update) | async-done | bytes 16777232 | tf_op jit(solution)/shard_map/all_gather | solution.py:36
  325.4 26.3 %gather_fusion = bf16[2304,2048]{1,0:T(8,128)(2,1)} fusion(bf16[4096,2048]{1,0:T(8,128)(2,1)} %bitcast.32, s32[3072]{0:T(1024)S(1)} %pad_clamp_fusion), kind=kCustom, calls=%fused_computation | custom fusion | bytes 18883584 | tf_op jit(solution)/shard_map/gather | solution.py:143
  351.7 5.4 %fusion.17 = f32[2304,256]{1,0:T(8,128)S(1)} fusion(bf16[2304,2048]{1,0:T(8,128)(2,1)} %gather_fusion, bf16[256,2048]{1,0:T(8,128)(2,1)S(1)} %copy-done), kind=kOutput, calls=%fused_computation.47 | convolution fusion | flops 2415919104 | bytes 12845056 | tf_op jit(solution)/shard_map/dot_general | solution.py:77
  357.2 0.3 broadcast_in_dim.6
  357.5 0.0 copy-start.6
  357.5 8.9 %all_to_all.15 = f32[2,2304,256]{2,1,0:T(8,128)} all-to-all(f32[2,2304,256]{2,1,0:T(8,128)S(1)} %broadcast_in_dim.6), channel_id=1, replica_groups=mesh['seq_0'=8,'seq_1'=2,'img_0'=4,'img_1'=2,'fsdp'=2] {'fsdp'}, dimensions={0} | all-to-all | bytes 9437184 | tf_op jit(solution)/shard_map/all_to_all | solution.py:19
  366.4 0.8 broadcast_in_dim.7
  367.2 3.8 all-to-all-start.2
  371.1 4.5 reduce_sum.66
  375.6 0.0 all-to-all-done.2
  375.6 0.0 slice-start.2
  375.6 6.8 %fusion.5 = (bf16[2304,256]{1,0:T(8,128)(2,1)}, f32[2304,256]{1,0:T(8,128)S(1)}) fusion(f32[2304,256]{1,0:T(8,128)} %reduce_sum.66, f32[256]{0:T(256)S(1)} %copy-done.11, bf16[2304,1024]{1,0:T(8,128)(2,1)} %bitcast.36, bf16[1024,256]{1,0:T(8,128)(2,1)S(1)} %bitcast.38), kind=kOutput, calls=%fused_computation.16 | convolution fusion | flops 1214447616 | bytes 11142144 | tf_op jit(solution)/shard_map/dot_general | solution.py:138
  382.4 4.0 fusion.6
  386.4 2.0 reshape_reshape.7
  388.4 3.6 fusion.18
  392.0 2.0 reshape_reshape.6
  393.9 2.7 pad_maximum_fusion
  396.6 3.6 reshape.221
  400.3 0.0 reduce-scatter.2.cloned.1.call-update
  400.3 9.0 %scatter_custom_fusion = f32[4096]{0:T(1024)S(1)} fusion(s32[2304]{0:T(1024)S(1)} %fusion.13, f32[2304]{0:T(1024)S(1)} %broadcast.124, f32[]{:T(128)} %constant.22.clone.1), kind=kCustom, calls=%fused_computation.37 | custom fusion | bytes 16388 | tf_op jit(solution)/shard_map/scatter | solution.py:116
  409.3 0.1 dynamic_slice.28
  409.4 0.2 fusion.7
  409.7 0.2 dynamic_update_slice.13
  409.9 6.3 %copy.20 = f32[2304,512]{1,0:T(8,128)} copy(f32[2304,512]{0,1:T(8,128)} %bitcast.35) | data formatting | bytes 9437184 | tf_op jit(solution)/shard_map/reshape | solution.py:87
  416.3 3.2 fusion.16
  419.5 0.1 reshape.229
  419.6 0.1 reshape.230
  419.7 0.1 reshape.227
  419.8 0.1 reshape.228
  419.9 0.2 convert_reduce_fusion.1
  420.1 0.3 dynamic_update_slice.12
  420.3 23.4 %all-reduce = (f32[4096]{0:T(1024)S(1)}, f32[4096]{0:T(1024)S(1)}, f32[1024]{0:T(1024)S(1)}, f32[1024]{0:T(1024)S(1)}) all-reduce(f32[4096]{0:T(1024)S(1)} %dynamic_update_slice.12, f32[4096]{0:T(1024)S(1)} %dynamic_update_slice.13, ...), channel_id=1, replica_groups=mesh['seq_0'=8,'seq_1'=2,'img_0'=4,'img_1'=2,'fsdp'=2] {'seq_0'}, use_global_device_ids=true, to_apply=%region_7.8 | all-reduce | flops 10240 | bytes 81920 | tf_op jit(solution)/shard_map/psum | solution.py:66
  443.8 6.2 %all-reduce.4 = (f32[4096]{0:T(1024)S(1)}, f32[4096]{0:T(1024)S(1)}, f32[1024]{0:T(1024)S(1)}, f32[1024]{0:T(1024)S(1)}) all-reduce(f32[4096]{0:T(1024)S(1)} %get-tuple-element.8, f32[4096]{0:T(1024)S(1)} %get-tuple-element.9, ...), channel_id=1, replica_groups=mesh['seq_0'=8,'seq_1'=2,'img_0'=4,'img_1'=2,'fsdp'=2] {'seq_1'}, use_global_device_ids=true, to_apply=%region_8.9 | all-reduce | flops 10240 | bytes 81920 | tf_op jit(solution)/shard_map/psum | solution.py:66
  449.9 14.1 %all-reduce.1 = (f32[4096]{0:T(1024)S(1)}, f32[4096]{0:T(1024)S(1)}, f32[1024]{0:T(1024)S(1)}, f32[1024]{0:T(1024)S(1)}) all-reduce(f32[4096]{0:T(1024)S(1)} %get-tuple-element.24, f32[4096]{0:T(1024)S(1)} %get-tuple-element.25, ...), channel_id=1, replica_groups=mesh['seq_0'=8,'seq_1'=2,'img_0'=4,'img_1'=2,'fsdp'=2] {'img_0'}, use_global_device_ids=true, to_apply=%region_9.10 | all-reduce | flops 10240 | bytes 81920 | tf_op jit(solution)/shard_map/psum | solution.py:66
  464.0 10.6 %all-reduce.3 = (f32[4096]{0:T(1024)S(1)}, f32[4096]{0:T(1024)S(1)}, f32[1024]{0:T(1024)S(1)}, f32[1024]{0:T(1024)S(1)}) all-reduce(f32[4096]{0:T(1024)S(1)} %get-tuple-element.12, f32[4096]{0:T(1024)S(1)} %get-tuple-element.13, ...), channel_id=1, replica_groups=mesh['seq_0'=8,'seq_1'=2,'img_0'=4,'img_1'=2,'fsdp'=2] {'img_1'}, use_global_device_ids=true, to_apply=%region_10.11 | all-reduce | flops 10240 | bytes 81920 | tf_op jit(solution)/shard_map/psum | solution.py:66
  474.6 15.7 %all-reduce.2 = (f32[4096]{0:T(1024)}, f32[4096]{0:T(1024)}, f32[1024]{0:T(1024)}, f32[1024]{0:T(1024)}) all-reduce(f32[4096]{0:T(1024)S(1)} %get-tuple-element.20, f32[4096]{0:T(1024)S(1)} %get-tuple-element.21, f32[1024]{0:T(1024)S(1)} %get-tuple-element.22, ...), channel_id=1, replica_groups=mesh['seq_0'=8,'seq_1'=2,'img_0'=4,'img_1'=2,'fsdp'=2] {'fsdp'}, use_global_device_ids=true, to_apply=%region_11.12 | all-reduce | flops 10240 | bytes 81920 | tf_op jit(solution)/shard_map/psum | solution.py:66
  490.3 1.0 slice.13
  491.3 0.7 reshape.223
  492.0 0.8 slice.12
  492.9 0.6 reshape.222
  (46 shorter events, 0.3 us)
Async XLA Ops:
  7.2 344.6 %copy-start = (bf16[256,2048]{1,0:T(8,128)(2,1)S(1)}, bf16[256,2048]{1,0:T(8,128)(2,1)}, u32[]{:S(2)}) copy-start(bf16[256,2048]{1,0:T(8,128)(2,1)} %param.14) | copy-start | bytes 3145732
  7.2 44.5 %copy-start.7 = (bf16[1,72,1024]{2,1,0:T(8,128)(2,1)S(1)}, bf16[1,72,1024]{2,1,0:T(8,128)(2,1)}, u32[]{:S(2)}) copy-start(bf16[1,72,1024]{2,1,0:T(8,128)(2,1)} %param.9) | copy-start | bytes 442372
  7.2 44.4 %all-gather.5.cloned.1.call-start = ((), (), s32[]{:S(2)}) async-start(), calls=%async_computation.5 | async-start | bytes 3145728 | tf_op jit(solution)/shard_map/all_gather | solution.py:36
  7.9 317.5 %all-gather.7.cloned.1.call-start = ((), (), s32[]{:S(2)}) async-start(), calls=%async_computation.6 | async-start | bytes 18874368 | tf_op jit(solution)/shard_map/all_gather | solution.py:36
  54.4 8.2 %copy-start.12 = (s32[1,2]{1,0:T(1,128)S(1)}, s32[1,2]{1,0:T(1,128)}, u32[]{:S(2)}) copy-start(s32[1,2]{1,0:T(1,128)} %param.16) | copy-start | bytes 28
  54.4 8.4 %copy-start.9 = (f32[1024]{0:T(1024)S(1)}, f32[1024]{0:T(1024)}, u32[]{:S(2)}) copy-start(f32[1024]{0:T(1024)} %param.10) | copy-start | bytes 12292
  54.4 8.5 %copy-start.8 = (f32[1024]{0:T(1024)S(1)}, f32[1024]{0:T(1024)}, u32[]{:S(2)}) copy-start(f32[1024]{0:T(1024)} %param.11) | copy-start | bytes 12292
  54.4 8.7 %copy-start.10 = (s32[1,2304]{1,0:T(1,128)S(1)}, s32[1,2304]{1,0:T(1,128)}, u32[]{:S(2)}) copy-start(s32[1,2304]{1,0:T(1,128)} %param.17) | copy-start | bytes 27652
  54.4 165.6 %all-to-all-start = ((bf16[32,72,1024]{2,1,0:T(8,128)(2,1)}), bf16[32,72,1024]{2,1,0:T(8,128)(2,1)}, u32[]{:S(2)}, u32[]{:S(2)}) async-start(bf16[32,72,1024]{2,1,0:T(8,128)(2,1)} %stack.3), calls=%async_computation | async-start | bytes 9437184 | tf_op jit(solution)/shard_map/all_to_all | solution.py:129
  270.1 6.9 %copy-start.1 = (f32[2304,8,2,64]{0,3,2,1:T(8,128)S(1)}, f32[2304,8,2,64]{0,3,2,1:T(8,128)}, u32[]{:S(2)}) copy-start(f32[2304,8,2,64]{0,3,2,1:T(8,128)} %copy.21) | copy-start | bytes 28311556
  357.5 8.9 %copy-start.6 = (bf16[512,256]{1,0:T(8,128)(2,1)S(1)}, bf16[512,256]{1,0:T(8,128)(2,1)}, u32[]{:S(2)}) copy-start(bf16[512,256]{1,0:T(8,128)(2,1)} %param.12) | copy-start | bytes 786436
  367.2 8.4 %all-to-all-start.2 = ((bf16[2,512,256]{2,1,0:T(8,128)(2,1)}), bf16[2,512,256]{2,1,0:T(8,128)(2,1)S(1)}, u32[]{:S(2)}, u32[]{:S(2)}) async-start(bf16[2,512,256]{2,1,0:T(8,128)(2,1)} %broadcast_in_dim.7), calls=%async_computation.2 | async-start | bytes 1048576 | tf_op jit(solution)/shard_map/all_to_all | solution.py:19
  371.1 4.5 copy-start.11
  371.1 119.2 %reduce-scatter.2.cloned.1.call-start = ((), (), s32[]{:S(2)}) async-start(), calls=%async_computation.4 | async-start | bytes 2949120 | tf_op jit(solution)/shard_map/reduce_scatter | solution.py:56
  371.1 11.3 %slice-start = ((s8[9437184]{0:T(1024)(128)(4,1)}), s8[1048576]{0:T(1024)(128)(4,1)S(1)}, s32[]{:S(2)}) async-start(s8[9437184]{0:T(1024)(128)(4,1)} %bitcast.33), calls=%async_computation.7 | async-start | bytes 2097152
  375.6 6.8 %copy-start.4 = (bf16[2,512,256]{2,1,0:T(8,128)(2,1)}, bf16[2,512,256]{2,1,0:T(8,128)(2,1)S(1)}, u32[]{:S(2)}) copy-start(bf16[2,512,256]{2,1,0:T(8,128)(2,1)S(1)} %all-to-all-done.2) | copy-start | bytes 1572868
  375.6 6.8 %slice-start.1 = ((s8[9437184]{0:T(1024)(128)(4,1)}), s8[4194304]{0:T(1024)(128)(4,1)S(1)}, s32[]{:S(2)}) async-start(s8[9437184]{0:T(1024)(128)(4,1)} %bitcast.33), calls=%async_computation.8 | async-start | bytes 8388608
  375.6 6.8 %slice-start.2 = ((s8[9437184]{0:T(1024)(128)(4,1)}), s8[4194304]{0:T(1024)(128)(4,1)S(1)}, s32[]{:S(2)}) async-start(s8[9437184]{0:T(1024)(128)(4,1)} %bitcast.33), calls=%async_computation.9 | async-start | bytes 8388608
  400.3 9.1 %copy-start.2 = (bf16[1,256,2048]{2,1,0:T(8,128)(2,1)S(1)}, bf16[1,256,2048]{2,1,0:T(8,128)(2,1)}, u32[]{:S(2)}) copy-start(bf16[1,256,2048]{2,1,0:T(8,128)(2,1)} %param.15) | copy-start | bytes 3145732
  400.3 9.6 %copy-start.5 = (bf16[2,512,256]{2,1,0:T(8,128)(2,1)S(1)}, bf16[2,512,256]{2,1,0:T(8,128)(2,1)}, u32[]{:S(2)}) copy-start(bf16[2,512,256]{2,1,0:T(8,128)(2,1)} %copy-done.4) | copy-start | bytes 1572868
  409.9 6.3 %copy-start.3 = (bf16[2304,256]{1,0:T(8,128)(2,1)S(1)}, bf16[2304,256]{1,0:T(8,128)(2,1)}, u32[]{:S(2)}) copy-start(bf16[2304,256]{1,0:T(8,128)(2,1)} %get-tuple-element.30) | copy-start | bytes 3538948
Sparse Core Ops, SparseCore 0:
  9.8 41.7 all-gather.4
  53.4 271.9 all-gather.6
  400.4 80.3 reduce-scatter.1
